TPU v7x, 32 devices: a whole 2x2x4 slice. The times are simulated.
32 devices in a mesh: mem: 4 (over x, core), lat: 8 (over z, y).
Axes of the slice: x: 2, y: 2, z: 4, core: 2. Of those that a mesh axis runs over, the one named last changes fastest.
Arguments:
- control: bfloat16 [8, 10, 704, 1440], P('mem', None, 'lat'), may hold values from -6 to 6
- perturb: bfloat16 [8, 10, 704, 1440], P('mem', None, None, 'lat'), may hold values from -6 to 6
- lon_loc: bfloat16 [1440, 1440], P(None, 'mem'), may hold values from 0 to 1, as said below
- lat_loc: bfloat16 [704, 704], P('mem'), may hold values from 0 to 1, as said below
- static_scale: float32 [10, 704, 1440], P(None, 'mem', 'lat'), may hold values from 0.3 to 1
- static_field: float32 [10, 704, 1440], P(None, 'mem', 'lat'), may hold values from -6 to 6
- courant: float32 [2, 704, 1440], P(None, 'mem', 'lat'), may hold values from -0.48 to 0.48
Outputs:
- increment: float32 [10, 704, 1440], P(None, 'mem', 'lat')
- evolved: float32 [10, 704, 1440], P(None, 'mem', 'lat')
Inputs may be any that keep to these rules, and one draw needn't show every extreme that they name: `lon_loc`: Symmetric, with positive entries. `lat_loc`: Symmetric, with positive entries.
All inputs are finite; a program needn't handle non-finite values.
Results may differ from a plain program's by a relative error of at most 0.0027.
Values may be sent and summed in bfloat16 or wider, within the bound.
No kernel may reach another device: no remote copies, remote signals or barrier semaphores. Data moves between devices by JAX's collectives and lax.ppermute only.
A program may use at most 128 MiB of HBM per device.

v0:
```python
import math
import jax
import jax.numpy as jnp
from jax import lax
from jax.sharding import PartitionSpec as P

NLAT = 704
STEPS = 4


def padded_2(shard, sides, width, wrap):
    for axis, dim in sides:
        size, length = (lax.axis_size(axis), shard.shape[dim])
        up = [(i, (i + 1) % size) for i in range(size if wrap else size - 1)]
        down = [(j, i) for i, j in up]
        last = lax.slice_in_dim(shard, length - width, length, axis=dim)
        leading = lax.slice_in_dim(shard, 0, width, axis=dim)
        before = lax.ppermute(last, axis, up)
        after = lax.ppermute(leading, axis, down)
        shard = jnp.concatenate([before, shard, after], axis=dim)
    return shard


def upwind(padded, east_west, north_south):
    center = padded[:, 1:-1, 1:-1]
    western = padded[:, 1:-1, :-2]
    eastern = padded[:, 1:-1, 2:]
    southern = padded[:, :-2, 1:-1]
    northern = padded[:, 2:, 1:-1]
    zonal = jnp.maximum(east_west, 0.0) * (center - western) + jnp.minimum(east_west, 0.0) * (
        eastern - center
    )
    meridional = jnp.maximum(north_south, 0.0) * (center - southern) + jnp.minimum(
        north_south, 0.0
    ) * (northern - center)
    return center - zonal - meridional


def lon_rim(values, width):
    return padded_2(values, (("lat", 2),), width, True)


def lat_rim(values, width):
    return padded_2(values, (("mem", 1),), width, False)


def evolve(current, courant):
    fields = current.shape[0]
    stacked = jnp.concatenate([current, courant], axis=0)
    extended = lat_rim(lon_rim(stacked, STEPS), STEPS)
    result = extended[:fields]
    wind_ext = extended[fields:]
    for step_index in range(STEPS):
        margin = step_index + 1
        inner_wind = wind_ext[
            :, margin : wind_ext.shape[1] - margin, margin : wind_ext.shape[2] - margin
        ]
        result = upwind(result, inner_wind[0], inner_wind[1])
    return result


def per_device(control, perturb, lon_loc, lat_loc, static_scale, static_field, courant):
    along_lon = jnp.einsum(
        "mfal,lc->amfc",
        control,
        lax.all_gather(lon_loc, "mem", axis=1, tiled=True),
        preferred_element_type=jnp.float32,
    ).astype(jnp.bfloat16)
    banded = lax.all_to_all(along_lon, "lat", split_axis=3, concat_axis=0, tiled=True)
    mem_here = banded.shape[1]
    fields = banded.shape[2]
    lon_width = banded.shape[3]
    flat_band = banded.reshape(banded.shape[0], mem_here * fields * lon_width)
    pert_rows = jnp.transpose(perturb, (2, 0, 1, 3))
    lat_weights_all = lax.all_gather(lat_loc, "mem", axis=0, tiled=True)
    members = mem_here * lax.axis_size("mem")
    ens_scale = 1.0 / math.sqrt(members - 1)
    rows_own = NLAT // lax.axis_size("mem")
    localized = jnp.dot(lat_weights_all, flat_band, preferred_element_type=jnp.float32)
    localized = localized.reshape(NLAT, mem_here, fields, lon_width)
    ensemble_all = jnp.transpose(
        lax.psum(jnp.sum(localized * pert_rows.astype(jnp.float32), axis=1) * ens_scale, "mem"),
        (1, 0, 2),
    )
    offset = lax.axis_index("mem") * rows_own
    ensemble = lax.dynamic_slice_in_dim(ensemble_all, offset, rows_own, 1)
    increment = ensemble + static_scale * static_field
    evolved = evolve(increment, courant)
    return (increment, evolved)


def solution(mesh):
    placed = (
        P("mem", None, "lat", None),
        P("mem", None, None, "lat"),
        P(None, "mem"),
        P("mem", None),
        P(None, "mem", "lat"),
        P(None, "mem", "lat"),
        P(None, "mem", "lat"),
    )
    return jax.shard_map(
        per_device,
        mesh=mesh,
        in_specs=placed,
        out_specs=(P(None, "mem", "lat"), P(None, "mem", "lat")),
        check_vma=False,
    )
```

profile of v0, /device:TPU:1, one launch (start us, length us, event | category | flops | bytes accessed | tf_op | source)
XLA Modules:
  0.0 472.6 jit_solution(8537434043374464706)
XLA Ops:
  7.2 0.0 all-gather.2.cloned.1.call-start
  7.2 2.4 copy.32
  9.6 38.8 %all-gather.2.cloned.1.call-done = bf16[1440,1440]{0,1:T(8,128)(2,1)} async-done(((bf16[1440,360]{0,1:T(8,128)(2,1)}), bf16[1440,1440]{0,1:T(8,128)(2,1)}) %all-gather.2.cloned.1.call-update) | async-done | bytes 4147216 | tf_op jit(solution)/shard_map/all_gather | solution.py:66
  48.4 13.5 %convert_bitcast_fusion = bf16[88,2,10,1440]{3,0,2,1:T(8,128)(2,1)} fusion(bf16[2,10,88,1440]{3,2,1,0:T(8,128)(2,1)} %param.7, bf16[1440,1440]{0,1:T(8,128)(2,1)} %all-gather.2.cloned.1.call-done), kind=kOutput, calls=%fused_computation.4 | convolution fusion | flops 7301606400 | bytes 14284800 | tf_op jit(solution)/shard_map/mfal,lc->amfc/dot_general | solution.py:63
  61.8 16.8 %copy.34 = bf16[88,2,10,1440]{0,1,2,3:T(2,128)(2,1)} copy(bf16[88,2,10,1440]{3,0,2,1:T(8,128)(2,1)} %convert_bitcast_fusion) | data formatting | bytes 10137600 | tf_op jit(solution)/shard_map/convert_element_type | solution.py:68
  78.6 5.4 %all-to-all-start = ((bf16[88,2,10,1440]{0,1,2,3:T(2,128)(2,1)}), bf16[88,2,10,1440]{0,1,2,3:T(2,128)(2,1)}, u32[]{:S(2)}, u32[]{:S(2)}) async-start(bf16[88,2,10,1440]{0,1,2,3:T(2,128)(2,1)} %copy.34), calls=%async_computation | async-start | bytes 14745600 | tf_op jit(solution)/shard_map/all_to_all | solution.py:69
  84.0 10.5 %all_gather.7 = bf16[704,704]{1,0:T(8,128)(2,1)S(1)} all-gather(bf16[176,704]{1,0:T(8,128)(2,1)S(1)} %copy-done.7), channel_id=1, replica_groups=mesh['mem'=4,'lat'=8] {'mem'}, dimensions={0}, use_global_device_ids=true | all-gather | bytes 1239040 | tf_op jit(solution)/shard_map/all_gather | solution.py:75
  94.5 150.4 %all-to-all-done = bf16[88,2,10,1440]{0,1,2,3:T(2,128)(2,1)} async-done(((bf16[88,2,10,1440]{0,1,2,3:T(2,128)(2,1)}), bf16[88,2,10,1440]{0,1,2,3:T(2,128)(2,1)}, u32[]{:S(2)}, u32[]{:S(2)}) %all-to-all-start) | async-done | bytes 5068832 | tf_op jit(solution)/shard_map/all_to_all | solution.py:69
  245.0 8.0 %copy.59 = bf16[88,2,10,8,180]{0,3,4,2,1:T(8,128)(2,1)} copy(bf16[88,2,10,8,180]{0,1,2,4,3:T(2,128)(2,1)} %bitcast.2) | data formatting | bytes 10137600 | tf_op jit(solution)/shard_map/all_to_all | solution.py:69
  253.0 12.2 %reshape.11 = bf16[704,3600]{0,1:T(8,128)(2,1)} reshape(bf16[8,88,2,10,180]{1,0,4,3,2:T(8,128)(2,1)} %bitcast.58) | data formatting | bytes 10137600 | tf_op jit(solution)/shard_map/reshape | solution.py:73
  265.2 9.6 %convolution_bitcast_fusion = f32[704,3600]{1,0:T(8,128)} fusion(bf16[704,3600]{0,1:T(8,128)(2,1)} %reshape.11, bf16[704,704]{1,0:T(8,128)(2,1)S(1)} %all_gather.7), kind=kOutput, calls=%fused_computation.3 | convolution fusion | flops 3568435200 | bytes 16197632 | tf_op jit(solution)/shard_map/dot_general | solution.py:79
  274.7 11.8 %copy.36 = f32[704,3600]{0,1:T(8,128)} copy(f32[704,3600]{1,0:T(8,128)} %convolution_bitcast_fusion) | data formatting | bytes 20275200 | tf_op jit(solution)/shard_map/dot_general | solution.py:79
  286.6 11.6 %reshape.12 = f32[704,2,10,180]{0,3,2,1:T(8,128)} reshape(f32[704,3600]{0,1:T(8,128)} %copy.36) | data formatting | bytes 20275200 | tf_op jit(solution)/shard_map/reshape | solution.py:80
  298.1 10.3 %fusion = f32[704,10,180]{0,2,1:T(8,128)} fusion(f32[704,2,10,180]{0,3,2,1:T(8,128)} %reshape.12, bf16[2,10,704,180]{2,0,3,1:T(2,128)(2,1)} %param.8), kind=kLoop, calls=%fused_computation.1 | loop fusion | flops 6336000 | bytes 20275200 | tf_op jit(solution)/shard_map/reduce_sum | solution.py:82
  308.4 5.5 %broadcast_multiply_fusion = f32[704,10,180]{0,2,1:T(8,128)} fusion(f32[704,10,180]{0,2,1:T(8,128)} %fusion), kind=kLoop, calls=%fused_computation.6 | loop fusion | flops 1267200 | bytes 10137600 | tf_op jit(solution)/shard_map/mul | solution.py:82
  314.0 1.5 copy-done.1
  315.4 1.8 copy.38
  317.3 3.0 copy.39
  320.3 0.2 copy.40
  320.5 101.5 %all-reduce.2.cloned.1.call-done = f32[704,10,180]{0,2,1:T(8,128)} async-done(((f32[704,10,180]{0,2,1:T(8,128)}), f32[704,10,180]{0,2,1:T(8,128)}) %all-reduce.2.cloned.1.call-update) | async-done | bytes 5068816 | tf_op jit(solution)/shard_map/psum | solution.py:82
  422.0 3.5 bitcast_add_fusion
  425.6 1.2 collective-permute-start
  426.8 3.0 collective-permute-start.1
  429.8 1.6 collective-permute-done
  431.6 0.3 pad_maximum_fusion
  431.8 1.4 fusion.34
  433.2 2.4 copy.45
  435.6 4.1 collective-permute-start.2
  439.7 1.1 copy.46
  440.8 2.1 collective-permute-start.3
  443.0 1.1 maximum_bitcast_fusion.7
  444.0 0.8 copy.49
  444.8 0.8 copy.50
  445.6 0.8 copy.51
  446.4 0.8 copy.52
  447.2 1.8 copy.53
  449.0 1.2 copy.47
  450.3 2.2 copy.48
  452.5 1.3 maximum_bitcast_fusion.3
  453.8 0.0 copy-done
  453.9 0.3 maximum_bitcast_fusion.5
  454.1 0.3 maximum_bitcast_fusion.1
  454.4 1.0 pad_maximum_fusion.1
  455.6 2.1 fusion.4
  457.7 2.0 fusion.28
  459.8 2.0 fusion.20
  461.8 2.1 fusion.12
  463.9 1.8 copy.54
  (28 shorter events, 0.3 us)
Async XLA Ops:
  7.2 41.2 %all-gather.2.cloned.1.call-start = ((), (), s32[]{:S(2)}) async-start(), calls=%async_computation.1 | async-start | bytes 5529600 | tf_op jit(solution)/shard_map/all_gather | solution.py:66
  78.6 5.4 %copy-start.7 = (bf16[176,704]{1,0:T(8,128)(2,1)S(1)}, bf16[176,704]{1,0:T(8,128)(2,1)}, u32[]{:S(2)}) copy-start(bf16[176,704]{1,0:T(8,128)(2,1)} %param.10) | copy-start | bytes 743428
  78.6 166.4 %all-to-all-start = ((bf16[88,2,10,1440]{0,1,2,3:T(2,128)(2,1)}), bf16[88,2,10,1440]{0,1,2,3:T(2,128)(2,1)}, u32[]{:S(2)}, u32[]{:S(2)}) async-start(bf16[88,2,10,1440]{0,1,2,3:T(2,128)(2,1)} %copy.34), calls=%async_computation | async-start | bytes 14745600 | tf_op jit(solution)/shard_map/all_to_all | solution.py:69
  84.0 338.0 %all-reduce.2.cloned.1.call-start = ((), (), s32[]{:S(2)}) async-start(), calls=%async_computation.2 | async-start | bytes 11304960 | tf_op jit(solution)/shard_map/psum | solution.py:82
  313.9 1.5 copy-start.1
  317.3 3.0 copy-start.2
  425.6 5.9 %collective-permute-start = (f32[12,176,4]{1,0,2:T(8,128)S(1)}, f32[12,176,4]{1,0,2:T(8,128)S(1)}, u32[]{:S(2)}, u32[]{:S(2)}) collective-permute-start(f32[12,176,4]{1,0,2:T(8,128)S(1)} %copy.41), channel_id=1, source_target_pairs={{0,1},{1,2},{2,3},{3,4},{4,5},{5,6},{6,7},{7,0},{8,9},{9,10},{10,1... | collective-permute-start | bytes 101384 | tf_op jit(solution)/shard_map/ppermute | solution.py:18
  426.8 4.7 collective-permute-start.1
  435.6 13.4 %collective-permute-start.2 = (f32[12,4,188]{2,1,0:T(4,128)}, f32[12,4,188]{2,1,0:T(4,128)}, u32[]{:S(2)}, u32[]{:S(2)}) collective-permute-start(f32[12,4,188]{2,1,0:T(4,128)} %copy.45), channel_id=1, source_target_pairs={{0,8},{8,16},{16,24},{1,9},{9,17},{17,25},{2,10},{10,18},{18,26},{... | collective-permute-start | bytes 108296 | tf_op jit(solution)/shard_map/ppermute | solution.py:18
  440.8 9.4 %collective-permute-start.3 = (f32[12,4,188]{2,1,0:T(4,128)}, f32[12,4,188]{2,1,0:T(4,128)}, u32[]{:S(2)}, u32[]{:S(2)}) collective-permute-start(f32[12,4,188]{2,1,0:T(4,128)} %copy.46), channel_id=1, source_target_pairs={{8,0},{16,8},{24,16},{9,1},{17,9},{25,17},{10,2},{18,10},{26,18},{... | collective-permute-start | bytes 108296 | tf_op jit(solution)/shard_map/ppermute | solution.py:19
  452.5 1.4 copy-start
  459.7 2.1 copy-start.3
  459.7 2.1 copy-start.4
  459.7 2.1 copy-start.5
  459.7 2.1 copy-start.6
Sparse Core Ops, SparseCore 0:
  10.1 38.2 all-gather.1
  314.1 107.8 all-reduce.1
where the time goes:
time: 474 us; the launch traced here: 473 us
  waiting for transfers between devices  292 us (62%)
  local copies, waits for them, and re-layouts  84.6 us (18%)
  other arithmetic  31.8 us (7%)
  matrix products  23 us (5%)
  starting transfers between devices  16 us (3%)
  between operations  14.3 us (3%)
  blocking collectives  10.5 us (2%)
    all_to_all x1, waiting for transfers between devices, per_device(): lax.all_to_all(along_lon, 'lat', split_axis=3, concat_axis=0, tiled=True)  150 us
    psum x1, waiting for transfers between devices, per_device(): lax.psum(jnp.sum(localized * pert_rows.astype(jnp.float32), axis=1) * ens...  102 us
    all_gather x1, waiting for transfers between devices, per_device(): lax.all_gather(lon_loc, 'mem', axis=1, tiled=True)  38.8 us
    convert_element_type x1, local copies, waits for them, and re-layouts, per_device(): along_lon = jnp.einsum('mfal,lc->amfc', control, lax.all_gather(lon_loc,...  16.8 us
    dot_general x1, matrix products, per_device(): jnp.einsum('mfal,lc->amfc', control, lax.all_gather(lon_loc, 'mem', axis=...  13.5 us
    unnamed x22, local copies, waits for them, and re-layouts  12.6 us
    reshape x1, local copies, waits for them, and re-layouts, per_device(): flat_band = banded.reshape(banded.shape[0], mem_here * fields * lon_width)  12.2 us
    dot_general x1, local copies, waits for them, and re-layouts, per_device(): jnp.dot(lat_weights_all, flat_band, preferred_element_type=jnp.float32)  11.8 us
  transfers between devices with their start and end apart: 7, of which 4 were waited for; matrix products, arithmetic and copies ran while one was open for 3% of the time, Pallas kernels for 0%

commit v1 on v0

--- a/solution.py
+++ b/solution.py
@@ -6,6 +6,21 @@
 
 NLAT = 704
 STEPS = 4
+
+
+def ring_apply(array, axis, dim, make, out_dim):
+    ways, here, step = (lax.axis_size(axis), lax.axis_index(axis), array.shape[dim])
+    results = []
+    for far in range(ways):
+        arriving = (
+            lax.ppermute(array, axis, [(d, (d + 1) % ways) for d in range(ways)])
+            if far + 1 < ways
+            else array
+        )
+        results.append(make(array, (here - far) % ways * step))
+        array = arriving
+    line = jnp.concatenate(results[::-1], axis=out_dim)
+    return jnp.roll(line, (here + 1) * results[0].shape[out_dim], axis=out_dim)
 
 
 def padded_2(shard, sides, width, wrap):
@@ -60,11 +75,14 @@
 
 
 def per_device(control, perturb, lon_loc, lat_loc, static_scale, static_field, courant):
-    along_lon = jnp.einsum(
-        "mfal,lc->amfc",
-        control,
-        lax.all_gather(lon_loc, "mem", axis=1, tiled=True),
-        preferred_element_type=jnp.float32,
+    along_lon = ring_apply(
+        lon_loc,
+        "mem",
+        1,
+        lambda own_block, start: jnp.einsum(
+            "mfal,lc->amfc", control, own_block, preferred_element_type=jnp.float32
+        ),
+        3,
     ).astype(jnp.bfloat16)
     banded = lax.all_to_all(along_lon, "lat", split_axis=3, concat_axis=0, tiled=True)
     mem_here = banded.shape[1]

time: 474 us -> 495 us (1.044)
  local copies, waits for them, and re-layouts: 84.6 us -> 107 us
  waiting for transfers between devices: 292 us -> 275 us
  starting transfers between devices: 16 us -> 23.8 us
  matrix products: 23 us -> 29 us
    all_gather x1 -> x0, waiting for transfers between devices: 38.8 us -> none  [per_device(): lax.all_gather(lon_loc, 'mem', axis=1, tiled=True)]
    ppermute x0 -> x3, waiting for transfers between devices: none -> 22.2 us  [ring_apply(): lax.ppermute(array, axis, [(d, (d + 1) % ways) for d in range(ways)])]
    concatenate x0 -> x1, local copies, waits for them, and re-layouts: none -> 16.7 us  [ring_apply(): return jnp.roll(line, (here + 1) * results[0].shape[out_dim], axis=out_dim)]
    convert_element_type x1 -> x2, local copies, waits for them, and re-layouts: 16.8 us -> 24.8 us  [per_device(): along_lon = ring_apply(lon_loc, 'mem', 1, lambda own_block, start: jnp.ei...]
    ppermute x0 -> x3, starting transfers between devices: none -> 7.6 us  [ring_apply(): lax.ppermute(array, axis, [(d, (d + 1) % ways) for d in range(ways)])]
    dot_general x1 -> x4, matrix products: 13.5 us -> 19.4 us  [per_device(): jnp.einsum('mfal,lc->amfc', control, own_block, preferred_element_type=jn...]
    unnamed x22 -> x25, local copies, waits for them, and re-layouts: 12.6 us -> 10.2 us
  transfers between devices with their start and end apart: 7 -> 9, of which waited for: 4 -> 6; matrix products, arithmetic and copies ran while one was open for 3% -> 6% of each run, Pallas kernels for 0% -> 0%
where the time goes in v1:
time: 495 us; the launch traced here: 492 us
  waiting for transfers between devices  275 us (56%)
  local copies, waits for them, and re-layouts  107 us (22%)
  other arithmetic  31.9 us (6%)
  matrix products  29 us (6%)
  starting transfers between devices  23.8 us (5%)
  between operations  14.3 us (3%)
  blocking collectives  11.8 us (2%)
    all_to_all x1, waiting for transfers between devices, per_device(): lax.all_to_all(along_lon, 'lat', split_axis=3, concat_axis=0, tiled=True)  148 us
    psum x1, waiting for transfers between devices, per_device(): lax.psum(jnp.sum(localized * pert_rows.astype(jnp.float32), axis=1) * ens...  103 us
    convert_element_type x2, local copies, waits for them, and re-layouts, per_device(): along_lon = ring_apply(lon_loc, 'mem', 1, lambda own_block, start: jnp.ei...  24.8 us
    ppermute x3, waiting for transfers between devices, ring_apply(): lax.ppermute(array, axis, [(d, (d + 1) % ways) for d in range(ways)])  22.2 us
    dot_general x4, matrix products, per_device(): jnp.einsum('mfal,lc->amfc', control, own_block, preferred_element_type=jn...  19.4 us
    concatenate x1, local copies, waits for them, and re-layouts, ring_apply(): return jnp.roll(line, (here + 1) * results[0].shape[out_dim], axis=out_dim)  16.7 us
    reshape x1, local copies, waits for them, and re-layouts, per_device(): flat_band = banded.reshape(banded.shape[0], mem_here * fields * lon_width)  12.2 us
    dot_general x1, local copies, waits for them, and re-layouts, per_device(): jnp.dot(lat_weights_all, flat_band, preferred_element_type=jnp.float32)  11.8 us
  transfers between devices with their start and end apart: 9, of which 6 were waited for; matrix products, arithmetic and copies ran while one was open for 6% of the time, Pallas kernels for 0%

profile of v1, /device:TPU:1, one launch (start us, length us, event | category | flops | bytes accessed | tf_op | source)
XLA Modules:
  0.0 492.3 jit_solution(2997312853463837)
XLA Ops:
  7.2 2.6 collective-permute-start
  9.8 12.7 %collective-permute-done = bf16[1440,360]{1,0:T(8,128)(2,1)S(1)} collective-permute-done((bf16[1440,360]{1,0:T(8,128)(2,1)}, bf16[1440,360]{1,0:T(8,128)(2,1)S(1)}, u32[]{:S(2)}, u32[]{:S(2)}) %collective-permute-start) | collective-permute-done | bytes 1036832 | tf_op jit(solution)/shard_map/ppermute | solution.py:16
  22.5 2.4 collective-permute-start.1
  24.9 6.0 %convolution_bitcast_fusion.1 = bf16[88,2,10,360]{3,0,2,1:T(8,128)(2,1)S(1)} fusion(bf16[2,10,88,1440]{3,2,1,0:T(8,128)(2,1)} %param.7, bf16[1440,360]{1,0:T(8,128)(2,1)} %param.9), kind=kOutput, calls=%fused_computation.57 | convolution fusion | flops 1824768000 | bytes 7372800 | tf_op jit(solution)/shard_map/mfal,lc->amfc/dot_general | solution.py:82
  30.8 6.4 %collective-permute-done.1 = bf16[1440,360]{1,0:T(8,128)(2,1)} collective-permute-done((bf16[1440,360]{1,0:T(8,128)(2,1)S(1)}, bf16[1440,360]{1,0:T(8,128)(2,1)}, u32[]{:S(2)}, u32[]{:S(2)}) %collective-permute-start.1) | collective-permute-done | bytes 1036832 | tf_op jit(solution)/shard_map/ppermute | solution.py:16
  37.2 2.6 collective-permute-start.2
  39.8 4.3 convolution_bitcast_fusion.2
  44.1 5.2 %convolution_bitcast_fusion.3 = bf16[88,2,10,360]{3,0,2,1:T(8,128)(2,1)} fusion(bf16[2,10,88,1440]{3,2,1,0:T(8,128)(2,1)S(1)} %copy-done.8, bf16[1440,360]{1,0:T(8,128)(2,1)} %collective-permute-done.1), kind=kOutput, calls=%fused_computation.59 | convolution fusion | flops 1824768000 | bytes 7372800 | tf_op jit(solution)/shard_map/mfal,lc->amfc/dot_general | solution.py:82
  49.3 3.1 collective-permute-done.2
  52.5 4.0 convolution_bitcast_fusion.4
  56.4 16.7 %concatenate.15 = bf16[88,2,10,2880]{3,0,2,1:T(8,128)(2,1)} concatenate(bf16[88,2,10,360]{3,0,2,1:T(8,128)(2,1)} %convolution_bitcast_fusion.4, bf16[88,2,10,360]{3,0,2,1:T(8,128)(2,1)} %convolution_bitcast_fusion.3, bf16[88,2,10,360]{3,0,2,1:T(8,128)(2,1)S(1)} %convolution_bitcast_fusion.2, bf16[88,2,10,360]{3,0,2,1:T(8,128)(2,1)S(1)} %convolution_bitcast_fusion.1, ...), dimensions={3} | concatenate | bytes 20275200 | tf_op jit(solution)/shard_map/jit(_roll_dynamic)/concatenate | solution.py:23
  73.2 7.9 %dynamic-slice_convert_fusion = bf16[88,2,10,1440]{3,0,2,1:T(8,128)(2,1)} fusion(bf16[88,2,10,2880]{3,0,2,1:T(8,128)(2,1)} %concatenate.15, s32[]{:T(128)S(6)} %select_n.17), kind=kLoop, calls=%fused_computation.2 | loop fusion | bytes 10137604 | tf_op jit(solution)/shard_map/convert_element_type | solution.py:86
  81.1 16.8 %copy.30 = bf16[88,2,10,1440]{0,1,2,3:T(2,128)(2,1)} copy(bf16[88,2,10,1440]{3,0,2,1:T(8,128)(2,1)} %dynamic-slice_convert_fusion) | data formatting | bytes 10137600 | tf_op jit(solution)/shard_map/convert_element_type | solution.py:86
  98.0 5.7 %all-to-all-start = ((bf16[88,2,10,1440]{0,1,2,3:T(2,128)(2,1)}), bf16[88,2,10,1440]{0,1,2,3:T(2,128)(2,1)}, u32[]{:S(2)}, u32[]{:S(2)}) async-start(bf16[88,2,10,1440]{0,1,2,3:T(2,128)(2,1)} %copy.30), calls=%async_computation | async-start | bytes 14745600 | tf_op jit(solution)/shard_map/all_to_all | solution.py:87
  103.7 11.8 %all_gather.3 = bf16[704,704]{1,0:T(8,128)(2,1)S(1)} all-gather(bf16[176,704]{1,0:T(8,128)(2,1)S(1)} %copy-done.7), channel_id=1, replica_groups=mesh['mem'=4,'lat'=8] {'mem'}, dimensions={0}, use_global_device_ids=true | all-gather | bytes 1239040 | tf_op jit(solution)/shard_map/all_gather | solution.py:93
  115.5 148.1 %all-to-all-done = bf16[88,2,10,1440]{0,1,2,3:T(2,128)(2,1)} async-done(((bf16[88,2,10,1440]{0,1,2,3:T(2,128)(2,1)}), bf16[88,2,10,1440]{0,1,2,3:T(2,128)(2,1)}, u32[]{:S(2)}, u32[]{:S(2)}) %all-to-all-start) | async-done | bytes 5068832 | tf_op jit(solution)/shard_map/all_to_all | solution.py:87
  263.6 8.0 %copy.57 = bf16[88,2,10,8,180]{0,3,4,2,1:T(8,128)(2,1)} copy(bf16[88,2,10,8,180]{0,1,2,4,3:T(2,128)(2,1)} %bitcast.12) | data formatting | bytes 10137600 | tf_op jit(solution)/shard_map/all_to_all | solution.py:87
  271.6 12.2 %reshape.11 = bf16[704,3600]{0,1:T(8,128)(2,1)} reshape(bf16[8,88,2,10,180]{1,0,4,3,2:T(8,128)(2,1)} %bitcast.84) | data formatting | bytes 10137600 | tf_op jit(solution)/shard_map/reshape | solution.py:91
  283.8 9.6 %convolution_bitcast_fusion = f32[704,3600]{1,0:T(8,128)} fusion(bf16[704,3600]{0,1:T(8,128)(2,1)} %reshape.11, bf16[704,704]{1,0:T(8,128)(2,1)S(1)} %all_gather.3), kind=kOutput, calls=%fused_computation.4 | convolution fusion | flops 3568435200 | bytes 16197632 | tf_op jit(solution)/shard_map/dot_general | solution.py:97
  293.4 11.8 %copy.32 = f32[704,3600]{0,1:T(8,128)} copy(f32[704,3600]{1,0:T(8,128)} %convolution_bitcast_fusion) | data formatting | bytes 20275200 | tf_op jit(solution)/shard_map/dot_general | solution.py:97
  305.2 11.6 %reshape.12 = f32[704,2,10,180]{0,3,2,1:T(8,128)} reshape(f32[704,3600]{0,1:T(8,128)} %copy.32) | data formatting | bytes 20275200 | tf_op jit(solution)/shard_map/reshape | solution.py:98
  316.8 10.3 %fusion = f32[704,10,180]{0,2,1:T(8,128)} fusion(f32[704,2,10,180]{0,3,2,1:T(8,128)} %reshape.12, bf16[2,10,704,180]{2,0,3,1:T(2,128)(2,1)} %param.8), kind=kLoop, calls=%fused_computation.1 | loop fusion | flops 6336000 | bytes 20275200 | tf_op jit(solution)/shard_map/reduce_sum | solution.py:100
  327.1 5.5 %broadcast_multiply_fusion = f32[704,10,180]{0,2,1:T(8,128)} fusion(f32[704,10,180]{0,2,1:T(8,128)} %fusion), kind=kLoop, calls=%fused_computation.5 | loop fusion | flops 1267200 | bytes 10137600 | tf_op jit(solution)/shard_map/mul | solution.py:100
  332.6 1.5 copy-done.1
  334.1 1.8 copy.34
  335.9 3.0 copy.35
  339.1 102.6 %all-reduce.2.cloned.1.call-done = f32[704,10,180]{0,2,1:T(8,128)} async-done(((f32[704,10,180]{0,2,1:T(8,128)}), f32[704,10,180]{0,2,1:T(8,128)}) %all-reduce.2.cloned.1.call-update) | async-done | bytes 5068816 | tf_op jit(solution)/shard_map/psum | solution.py:100
  441.7 3.5 bitcast_add_fusion
  445.2 1.2 collective-permute-start.3
  446.5 3.0 collective-permute-start.4
  449.5 1.6 collective-permute-done.3
  451.5 1.4 fusion.37
  452.9 2.4 copy.41
  455.3 4.1 collective-permute-start.5
  459.4 1.1 copy.42
  460.5 2.1 collective-permute-start.6
  462.7 1.1 maximum_bitcast_fusion.7
  463.7 0.8 copy.45
  466.9 1.8 copy.49
  468.7 1.2 copy.43
  469.9 2.2 copy.44
  472.2 1.3 maximum_bitcast_fusion.3
  474.1 1.0 pad_maximum_fusion.1
  475.3 2.1 fusion.3
  477.4 2.0 fusion.27
  479.5 2.1 fusion.19
  481.6 2.1 fusion.11
  483.6 1.8 copy.50
  (39 shorter events, 3.7 us)
Async XLA Ops:
  7.2 15.3 %collective-permute-start = (bf16[1440,360]{1,0:T(8,128)(2,1)}, bf16[1440,360]{1,0:T(8,128)(2,1)S(1)}, u32[]{:S(2)}, u32[]{:S(2)}) collective-permute-start(bf16[1440,360]{1,0:T(8,128)(2,1)} %param.9), channel_id=1, source_target_pairs={{0,8},{8,16},{16,24},{24,0},{1,9},{9,17},{17,25},{25,1},{2,10},{10... | collective-permute-start | bytes 3110408 | tf_op jit(solution)/shard_map/ppermute | solution.py:16
  22.5 8.4 %copy-start.9 = (bf16[1440,360]{1,0:T(8,128)(2,1)}, bf16[1440,360]{1,0:T(8,128)(2,1)S(1)}, u32[]{:S(2)}) copy-start(bf16[1440,360]{1,0:T(8,128)(2,1)S(1)} %collective-permute-done) | copy-start | bytes 3110404
  22.5 14.7 %collective-permute-start.1 = (bf16[1440,360]{1,0:T(8,128)(2,1)S(1)}, bf16[1440,360]{1,0:T(8,128)(2,1)}, u32[]{:S(2)}, u32[]{:S(2)}) collective-permute-start(bf16[1440,360]{1,0:T(8,128)(2,1)S(1)} %collective-permute-done), channel_id=1, source_target_pairs={{0,8},{8,16},{16,24},{24,0},{1,9},{9,17},{17,25},{25,1},{2,10},{10... | collective-permute-start | bytes 3110408 | tf_op jit(solution)/shard_map/ppermute | solution.py:16
  24.9 14.9 %copy-start.8 = (bf16[2,10,88,1440]{3,2,1,0:T(8,128)(2,1)S(1)}, bf16[2,10,88,1440]{3,2,1,0:T(8,128)(2,1)}, u32[]{:S(2)}) copy-start(bf16[2,10,88,1440]{3,2,1,0:T(8,128)(2,1)} %param.7) | copy-start | bytes 15206404
  37.2 15.3 %collective-permute-start.2 = (bf16[1440,360]{1,0:T(8,128)(2,1)}, bf16[1440,360]{1,0:T(8,128)(2,1)S(1)}, u32[]{:S(2)}, u32[]{:S(2)}) collective-permute-start(bf16[1440,360]{1,0:T(8,128)(2,1)} %collective-permute-done.1), channel_id=1, source_target_pairs={{0,8},{8,16},{16,24},{24,0},{1,9},{9,17},{17,25},{25,1},{2,10},{10... | collective-permute-start | bytes 3110408 | tf_op jit(solution)/shard_map/ppermute | solution.py:16
  98.0 5.7 %copy-start.7 = (bf16[176,704]{1,0:T(8,128)(2,1)S(1)}, bf16[176,704]{1,0:T(8,128)(2,1)}, u32[]{:S(2)}) copy-start(bf16[176,704]{1,0:T(8,128)(2,1)} %param.10) | copy-start | bytes 743428
  98.0 165.7 %all-to-all-start = ((bf16[88,2,10,1440]{0,1,2,3:T(2,128)(2,1)}), bf16[88,2,10,1440]{0,1,2,3:T(2,128)(2,1)}, u32[]{:S(2)}, u32[]{:S(2)}) async-start(bf16[88,2,10,1440]{0,1,2,3:T(2,128)(2,1)} %copy.30), calls=%async_computation | async-start | bytes 14745600 | tf_op jit(solution)/shard_map/all_to_all | solution.py:87
  103.6 338.1 %all-reduce.2.cloned.1.call-start = ((), (), s32[]{:S(2)}) async-start(), calls=%async_computation.1 | async-start | bytes 11304960 | tf_op jit(solution)/shard_map/psum | solution.py:100
  332.6 1.5 copy-start.1
  335.9 3.0 copy-start.2
  445.2 5.9 %collective-permute-start.3 = (f32[12,176,4]{1,0,2:T(8,128)S(1)}, f32[12,176,4]{1,0,2:T(8,128)S(1)}, u32[]{:S(2)}, u32[]{:S(2)}) collective-permute-start(f32[12,176,4]{1,0,2:T(8,128)S(1)} %copy.37), channel_id=1, source_target_pairs={{0,1},{1,2},{2,3},{3,4},{4,5},{5,6},{6,7},{7,0},{8,9},{9,10},{10,1... | collective-permute-start | bytes 101384 | tf_op jit(solution)/shard_map/ppermute | solution.py:33
  446.5 4.7 collective-permute-start.4
  455.3 13.4 %collective-permute-start.5 = (f32[12,4,188]{2,1,0:T(4,128)}, f32[12,4,188]{2,1,0:T(4,128)}, u32[]{:S(2)}, u32[]{:S(2)}) collective-permute-start(f32[12,4,188]{2,1,0:T(4,128)} %copy.41), channel_id=1, source_target_pairs={{0,8},{8,16},{16,24},{1,9},{9,17},{17,25},{2,10},{10,18},{18,26},{... | collective-permute-start | bytes 108296 | tf_op jit(solution)/shard_map/ppermute | solution.py:33
  460.5 9.4 %collective-permute-start.6 = (f32[12,4,188]{2,1,0:T(4,128)}, f32[12,4,188]{2,1,0:T(4,128)}, u32[]{:S(2)}, u32[]{:S(2)}) collective-permute-start(f32[12,4,188]{2,1,0:T(4,128)} %copy.42), channel_id=1, source_target_pairs={{8,0},{16,8},{24,16},{9,1},{17,9},{25,17},{10,2},{18,10},{26,18},{... | collective-permute-start | bytes 108296 | tf_op jit(solution)/shard_map/ppermute | solution.py:34
  472.2 1.4 copy-start
  479.4 2.1 copy-start.3
  479.4 2.1 copy-start.4
  479.4 2.1 copy-start.5
  479.4 2.1 copy-start.6
Sparse Core Ops, SparseCore 0:
  332.8 108.8 all-reduce.1
